TPU v7x, 32 devices: a whole 2x2x4 slice. The times are simulated.
32 devices in a mesh: dp: 8 (over z, y), tensor: 4 (over x, core).
Axes of the slice: x: 2, y: 2, z: 4, core: 2. Of those that a mesh axis runs over, the one named last changes fastest.
Arguments:
- tokens: bfloat16 [8192, 2048], P(('dp', 'tensor')), may hold values from -6 to 6
- norm_gain: bfloat16 [2048], replicated, may hold values from 0.5 to 1.5
- norm_bias: bfloat16 [2048], replicated, may hold values from -3 to 3
- query_weight: bfloat16 [2048, 2048], P('dp', 'tensor'), may hold values from -0.1875 to 0.1875
- query_bias: bfloat16 [2048], P('tensor'), may hold values from -3 to 3
- key_weight: bfloat16 [2048, 2048], P('dp', 'tensor'), may hold values from -0.1875 to 0.1875
- key_bias: bfloat16 [2048], P('tensor'), may hold values from -3 to 3
- value_weight: bfloat16 [2048, 2048], P('dp', 'tensor'), may hold values from -0.125 to 0.125
- value_bias: bfloat16 [2048], P('tensor'), may hold values from -3 to 3
- output_weight: bfloat16 [2048, 2048], P('tensor', 'dp'), may hold values from -0.5 to 0.5
- output_bias: bfloat16 [2048], replicated, may hold values from -3 to 3
- up_weight: bfloat16 [2048, 8192], P('dp', 'tensor'), may hold values from -0.125 to 0.125
- up_bias: bfloat16 [8192], P('tensor'), may hold values from -3 to 3
- down_weight: bfloat16 [8192, 2048], P('tensor', 'dp'), may hold values from -0.0625 to 0.0625
- down_bias: bfloat16 [2048], replicated, may hold values from -3 to 3
- doc_split: int32 [8], P('dp'), may hold values from 256 to 768, as said below
- cotangent: bfloat16 [8192, 2048], P(('dp', 'tensor')), may hold values from -6 to 6
Outputs:
- out: bfloat16 [8192, 2048], P(('dp', 'tensor'))
- grad_tokens: float32 [8192, 2048], P(('dp', 'tensor'))
- grad_norm_gain: float32 [2048], replicated
- grad_norm_bias: float32 [2048], replicated
- grad_query_weight: float32 [2048, 2048], P('dp', 'tensor')
- grad_query_bias: float32 [2048], P('tensor')
- grad_key_weight: float32 [2048, 2048], P('dp', 'tensor')
- grad_key_bias: float32 [2048], P('tensor')
- grad_value_weight: float32 [2048, 2048], P('dp', 'tensor')
- grad_value_bias: float32 [2048], P('tensor')
- grad_output_weight: float32 [2048, 2048], P('tensor', 'dp')
- grad_output_bias: float32 [2048], replicated
- grad_up_weight: float32 [2048, 8192], P('dp', 'tensor')
- grad_up_bias: float32 [8192], P('tensor')
- grad_down_weight: float32 [8192, 2048], P('tensor', 'dp')
- grad_down_bias: float32 [2048], replicated
Inputs may be any that keep to these rules, and one draw needn't show every extreme that they name: `doc_split`: each sequence holds two documents; the second begins at a multiple of 256, and every such start from 256 to 768 occurs in some sequence.
All inputs are finite; a program needn't handle non-finite values.
Results may differ from a plain program's by a relative error of at most 0.013.
The roundings to bfloat16 on the way count: a program that leaves them out, or rounds other values in their place, can miss the bound.
Values may be sent and summed in bfloat16 or wider, within the bound.
A program may use at most 256 MiB of HBM per device.

v0:
```python
import jax
import jax.numpy as jnp
from jax import lax
from jax.sharding import PartitionSpec as P

HEADS = 32
HEAD_DIM = 64
ROT = 32
BLOCK = 256
SEQ = 1024
EPS = 1e-05
NEG = -1000000000.0


def tables(split_at, seq_len):
    token_index = jnp.arange(seq_len, dtype=jnp.int32)
    later_doc = token_index >= split_at
    position = (token_index - jnp.where(later_doc, split_at, 0)).astype(jnp.float32)
    frequency = 10000.0 ** (-(2.0 * jnp.arange(ROT // 2, dtype=jnp.float32)) / ROT)
    angles = position[:, None] * frequency[None, :]
    return (jnp.cos(angles), jnp.sin(angles), later_doc)


def rotate(values, cosine, sine_table):
    half_rot = ROT // 2
    front_part = values[..., :half_rot]
    back_part = values[..., half_rot:ROT]
    cos_wide = cosine[..., None, :]
    sin_wide = sine_table[..., None, :]
    return jnp.concatenate(
        [
            front_part * cos_wide - back_part * sin_wide,
            back_part * cos_wide + front_part * sin_wide,
            values[..., ROT:],
        ],
        axis=-1,
    )


def rotate_back(grads, cosine, sine_table):
    half_rot = ROT // 2
    front_part = grads[..., :half_rot]
    back_part = grads[..., half_rot:ROT]
    cos_wide = cosine[..., None, :]
    sin_wide = sine_table[..., None, :]
    return jnp.concatenate(
        [
            front_part * cos_wide + back_part * sin_wide,
            back_part * cos_wide - front_part * sin_wide,
            grads[..., ROT:],
        ],
        axis=-1,
    )


def contract_last(left, right):
    return lax.dot_general(
        left, right, (((1,), (1,)), ((), ())), preferred_element_type=jnp.float32
    )


def contract_first(left, right):
    return lax.dot_general(
        left, right, (((0,), (0,)), ((), ())), preferred_element_type=jnp.float32
    )


def block_layout(split_at, seq_len):
    token_index = jnp.arange(seq_len, dtype=jnp.int32)
    return (token_index // BLOCK, token_index >= split_at)


def attend(queries, keys_rot, values_all, split_at):
    seq_len, heads_here, head_size = queries.shape
    rows_step = min(512, seq_len)
    step_count = seq_len // rows_step
    block_ids, later_doc = block_layout(split_at, seq_len)
    scale = HEAD_DIM ** (-0.5)

    def one_block(block_item):
        query_rows, row_blocks, row_docs = block_item
        allowed = (block_ids[None, :] <= row_blocks[:, None]) & (
            later_doc[None, :] == row_docs[:, None]
        )
        raw_scores = jnp.einsum(
            "qhd,khd->hqk", query_rows, keys_rot, preferred_element_type=jnp.float32
        )
        scores = jnp.where(allowed[None], raw_scores * scale, NEG)
        row_top = jnp.max(scores, -1, keepdims=True)
        exponent = jnp.exp(scores - row_top)
        row_total = jnp.sum(exponent, -1, keepdims=True)
        probability = (exponent / row_total).astype(jnp.bfloat16)
        attended = jnp.einsum(
            "hqk,khd->qhd", probability, values_all, preferred_element_type=jnp.float32
        )
        return (attended.astype(jnp.bfloat16), (row_top + jnp.log(row_total))[..., 0])

    attended, log_totals = lax.map(
        one_block,
        (
            queries.reshape(step_count, rows_step, heads_here, head_size),
            block_ids.reshape(step_count, rows_step),
            later_doc.reshape(step_count, rows_step),
        ),
    )
    return (attended.reshape(seq_len, heads_here, head_size), log_totals)


def attend_back(queries, keys_rot, values_all, grad_attended, log_totals, split_at):
    seq_len, heads_here, head_size = queries.shape
    rows_step = min(512, seq_len)
    step_count = seq_len // rows_step
    block_ids, later_doc = block_layout(split_at, seq_len)
    scale = HEAD_DIM ** (-0.5)

    def one_block(running, block_item):
        key_acc, value_acc = running
        query_rows, grad_rows, log_rows, row_blocks, row_docs = block_item
        allowed = (block_ids[None, :] <= row_blocks[:, None]) & (
            later_doc[None, :] == row_docs[:, None]
        )
        raw_scores = jnp.einsum(
            "qhd,khd->hqk", query_rows, keys_rot, preferred_element_type=jnp.float32
        )
        scores = jnp.where(allowed[None], raw_scores * scale, NEG)
        probability = jnp.exp(scores - log_rows[..., None])
        grad_prob = jnp.einsum(
            "qhd,khd->hqk", grad_rows, values_all, preferred_element_type=jnp.float32
        )
        row_dot = jnp.sum(probability * grad_prob, -1, keepdims=True)
        grad_scores = (probability * (grad_prob - row_dot) * scale).astype(jnp.bfloat16)
        grad_query = jnp.einsum(
            "hqk,khd->qhd", grad_scores, keys_rot, preferred_element_type=jnp.float32
        )
        key_acc = key_acc + jnp.einsum(
            "hqk,qhd->khd", grad_scores, query_rows, preferred_element_type=jnp.float32
        )
        value_acc = value_acc + jnp.einsum(
            "hqk,qhd->khd",
            probability.astype(jnp.bfloat16),
            grad_rows,
            preferred_element_type=jnp.float32,
        )
        return ((key_acc, value_acc), grad_query)

    zeros_kv = jnp.zeros((seq_len, heads_here, head_size), jnp.float32)
    (grad_keys, grad_values), grad_queries = lax.scan(
        one_block,
        (zeros_kv, zeros_kv),
        (
            queries.reshape(step_count, rows_step, heads_here, head_size),
            grad_attended.reshape(step_count, rows_step, heads_here, head_size),
            log_totals,
            block_ids.reshape(step_count, rows_step),
            later_doc.reshape(step_count, rows_step),
        ),
    )
    return (grad_queries.reshape(seq_len, heads_here, head_size), grad_keys, grad_values)


def gelu_tanh(hidden):
    return jax.nn.gelu(hidden, approximate=True)


def on_device(
    tokens,
    norm_gain,
    norm_bias,
    query_weight,
    query_bias,
    key_weight,
    key_bias,
    value_weight,
    value_bias,
    output_weight,
    output_bias,
    up_weight,
    up_bias,
    down_weight,
    down_bias,
    doc_split,
    cotangent,
):
    heads_here = HEADS // lax.axis_size("tensor")
    width_here = heads_here * HEAD_DIM
    seq_count = doc_split.shape[0]
    gain_wide = norm_gain.astype(jnp.float32)
    tokens_wide = tokens.astype(jnp.float32)
    row_mean = jnp.mean(tokens_wide, -1, keepdims=True)
    centred = tokens_wide - row_mean
    inv_scale = lax.rsqrt(jnp.mean(centred * centred, -1, keepdims=True) + EPS)
    standard = centred * inv_scale
    normed = (standard * gain_wide + norm_bias.astype(jnp.float32)).astype(jnp.bfloat16)
    normed_all = lax.all_gather(normed, "tensor", axis=0, tiled=True)
    full_query, full_key, full_value, full_up = (
        lax.all_gather(query_weight, "dp", axis=0, tiled=True),
        lax.all_gather(key_weight, "dp", axis=0, tiled=True),
        lax.all_gather(value_weight, "dp", axis=0, tiled=True),
        lax.all_gather(up_weight, "dp", axis=0, tiled=True),
    )
    full_output, full_down = (
        lax.all_gather(output_weight, "dp", axis=1, tiled=True),
        lax.all_gather(down_weight, "dp", axis=1, tiled=True),
    )
    rows_all = normed_all.shape[0]
    q_pre = jnp.dot(normed_all, full_query, preferred_element_type=jnp.float32) + query_bias.astype(
        jnp.float32
    )
    k_pre = jnp.dot(normed_all, full_key, preferred_element_type=jnp.float32) + key_bias.astype(
        jnp.float32
    )
    v_pre = jnp.dot(normed_all, full_value, preferred_element_type=jnp.float32) + value_bias.astype(
        jnp.float32
    )
    hidden = jnp.dot(normed_all, full_up, preferred_element_type=jnp.float32) + up_bias.astype(
        jnp.float32
    )
    cosine, sine_table, later_unused = jax.vmap(lambda split_at: tables(split_at, SEQ))(doc_split)
    shaped = (seq_count, SEQ, heads_here, HEAD_DIM)
    queries = rotate(q_pre.reshape(shaped), cosine, sine_table).astype(jnp.bfloat16)
    keys_rot = rotate(k_pre.reshape(shaped), cosine, sine_table).astype(jnp.bfloat16)
    values_all = v_pre.astype(jnp.bfloat16).reshape(shaped)
    attended, log_totals = lax.map(
        lambda seq_item: attend(*seq_item), (queries, keys_rot, values_all, doc_split)
    )
    attended_flat = attended.reshape(rows_all, width_here)
    activated = gelu_tanh(hidden).astype(jnp.bfloat16)
    partial_out = jnp.dot(attended_flat, full_output, preferred_element_type=jnp.float32) + jnp.dot(
        activated, full_down, preferred_element_type=jnp.float32
    )
    mixed = lax.psum_scatter(
        partial_out.astype(jnp.bfloat16), "tensor", scatter_dimension=0, tiled=True
    ).astype(jnp.float32)
    out_bias = output_bias.astype(jnp.float32) + down_bias.astype(jnp.float32)
    out = (tokens_wide + mixed + out_bias).astype(jnp.bfloat16)
    cot_all = lax.all_gather(cotangent, "tensor", axis=0, tiled=True)
    grad_attn_wide = contract_last(cot_all, full_output)
    grad_activated = contract_last(cot_all, full_down)
    grad_attn = grad_attn_wide.astype(jnp.bfloat16)
    grad_hidden = jax.vjp(gelu_tanh, hidden)[1](grad_activated)[0].astype(jnp.bfloat16)
    grad_queries, grad_keys, grad_values = lax.map(
        lambda seq_item: attend_back(*seq_item),
        (queries, keys_rot, values_all, grad_attn.reshape(shaped), log_totals, doc_split),
    )
    grad_q = (
        rotate_back(grad_queries, cosine, sine_table)
        .reshape(rows_all, width_here)
        .astype(jnp.bfloat16)
    )
    grad_k = (
        rotate_back(grad_keys, cosine, sine_table)
        .reshape(rows_all, width_here)
        .astype(jnp.bfloat16)
    )
    grad_v = grad_values.reshape(rows_all, width_here).astype(jnp.bfloat16)
    grad_normed_part = (
        contract_last(grad_q, full_query)
        + contract_last(grad_k, full_key)
        + contract_last(grad_v, full_value)
        + contract_last(grad_hidden, full_up)
    )
    grad_normed = lax.psum_scatter(
        grad_normed_part.astype(jnp.bfloat16), "tensor", scatter_dimension=0, tiled=True
    ).astype(jnp.float32)
    grad_query_weight, grad_key_weight, grad_value_weight, grad_up_weight = (
        lax.psum_scatter(
            contract_first(normed_all, grad_q).astype(jnp.bfloat16),
            "dp",
            scatter_dimension=0,
            tiled=True,
        ).astype(jnp.float32),
        lax.psum_scatter(
            contract_first(normed_all, grad_k).astype(jnp.bfloat16),
            "dp",
            scatter_dimension=0,
            tiled=True,
        ).astype(jnp.float32),
        lax.psum_scatter(
            contract_first(normed_all, grad_v).astype(jnp.bfloat16),
            "dp",
            scatter_dimension=0,
            tiled=True,
        ).astype(jnp.float32),
        lax.psum_scatter(
            contract_first(normed_all, grad_hidden).astype(jnp.bfloat16),
            "dp",
            scatter_dimension=0,
            tiled=True,
        ).astype(jnp.float32),
    )
    grad_output_weight, grad_down_weight = (
        lax.psum_scatter(
            contract_first(attended_flat, cot_all).astype(jnp.bfloat16),
            "dp",
            scatter_dimension=1,
            tiled=True,
        ).astype(jnp.float32),
        lax.psum_scatter(
            contract_first(activated, cot_all).astype(jnp.bfloat16),
            "dp",
            scatter_dimension=1,
            tiled=True,
        ).astype(jnp.float32),
    )
    grad_query_bias, grad_key_bias, grad_value_bias, grad_up_bias = lax.psum(
        (
            jnp.sum(grad_q, 0, dtype=jnp.float32),
            jnp.sum(grad_k, 0, dtype=jnp.float32),
            jnp.sum(grad_v, 0, dtype=jnp.float32),
            jnp.sum(grad_hidden, 0, dtype=jnp.float32),
        ),
        "dp",
    )
    cot_wide = cotangent.astype(jnp.float32)
    grad_scaled = grad_normed * gain_wide
    grad_tokens = cot_wide + inv_scale * (
        grad_scaled
        - jnp.mean(grad_scaled, -1, keepdims=True)
        - standard * jnp.mean(grad_scaled * standard, -1, keepdims=True)
    )
    grad_norm_gain, grad_norm_bias, grad_out_bias = lax.psum(
        (jnp.sum(grad_normed * standard, 0), jnp.sum(grad_normed, 0), jnp.sum(cot_wide, 0)),
        ("dp", "tensor"),
    )
    return (
        out,
        grad_tokens,
        grad_norm_gain,
        grad_norm_bias,
        grad_query_weight,
        grad_query_bias,
        grad_key_weight,
        grad_key_bias,
        grad_value_weight,
        grad_value_bias,
        grad_output_weight,
        grad_out_bias,
        grad_up_weight,
        grad_up_bias,
        grad_down_weight,
        grad_out_bias,
    )


def solution(mesh):
    in_specs = (
        P(("dp", "tensor"), None),
        P(),
        P(),
        P("dp", "tensor"),
        P("tensor"),
        P("dp", "tensor"),
        P("tensor"),
        P("dp", "tensor"),
        P("tensor"),
        P("tensor", "dp"),
        P(),
        P("dp", "tensor"),
        P("tensor"),
        P("tensor", "dp"),
        P(),
        P("dp"),
        P(("dp", "tensor"), None),
    )
    out_specs = (
        P(("dp", "tensor"), None),
        P(("dp", "tensor"), None),
        P(),
        P(),
        P("dp", "tensor"),
        P("tensor"),
        P("dp", "tensor"),
        P("tensor"),
        P("dp", "tensor"),
        P("tensor"),
        P("tensor", "dp"),
        P(),
        P("dp", "tensor"),
        P("tensor"),
        P("tensor", "dp"),
        P(),
    )
    return jax.shard_map(
        on_device, mesh=mesh, in_specs=in_specs, out_specs=out_specs, check_vma=False
    )
```

profile of v0, /device:TPU:0, one launch (start us, length us, event | category | flops | bytes accessed | tf_op | source)
XLA Modules:
  0.0 1225.4 jit_solution(8028844312723084863)
XLA Ops:
  20.9 41.0 %all-gather.11.cloned.1.call-done = bf16[2048,512]{1,0:T(8,128)(2,1)} async-done(((bf16[256,512]{1,0:T(8,128)(2,1)}), bf16[2048,512]{1,0:T(8,128)(2,1)}) %all-gather.11.cloned.1.call-update) | async-done | bytes 2097168 | tf_op jit(solution)/shard_map/all_gather | solution.py:196
  62.0 35.1 %all-gather.9.cloned.1.call-done = bf16[1024,2048]{1,0:T(8,128)(2,1)} async-done(((bf16[256,2048]{1,0:T(8,128)(2,1)}), bf16[1024,2048]{1,0:T(8,128)(2,1)}) %all-gather.9.cloned.1.call-update) | async-done | bytes 4194320 | tf_op jit(solution)/shard_map/all_gather | solution.py:194
  97.1 5.2 convolution_add_fusion.1
  102.4 45.9 %all-gather.13.cloned.1.call-done = bf16[2048,512]{1,0:T(8,128)(2,1)} async-done(((bf16[256,512]{1,0:T(8,128)(2,1)}), bf16[2048,512]{1,0:T(8,128)(2,1)}) %all-gather.13.cloned.1.call-update) | async-done | bytes 2097168 | tf_op jit(solution)/shard_map/all_gather | solution.py:197
  148.4 5.2 convolution_add_fusion
  158.0 41.2 %all-gather.17.cloned.1.call-done = bf16[512,2048]{1,0:T(8,128)(2,1)} async-done(((bf16[512,256]{1,0:T(8,128)(2,1)}), bf16[512,2048]{1,0:T(8,128)(2,1)}) %all-gather.17.cloned.1.call-update) | async-done | bytes 2097168 | tf_op jit(solution)/shard_map/all_gather | solution.py:202
  199.2 34.1 %all-gather.23.cloned.1.call-done = bf16[1024,2048]{1,0:T(8,128)(2,1)} async-done(((bf16[256,2048]{1,0:T(8,128)(2,1)}), bf16[1024,2048]{1,0:T(8,128)(2,1)}) %all-gather.23.cloned.1.call-update) | async-done | bytes 4194320 | tf_op jit(solution)/shard_map/all_gather | solution.py:236
  233.2 6.2 convolution_convert_fusion.6
  248.4 36.0 %all-gather.15.cloned.1.call-done = bf16[2048,512]{1,0:T(8,128)(2,1)} async-done(((bf16[256,512]{1,0:T(8,128)(2,1)}), bf16[2048,512]{1,0:T(8,128)(2,1)}) %all-gather.15.cloned.1.call-update) | async-done | bytes 2097168 | tf_op jit(solution)/shard_map/all_gather | solution.py:198
  284.4 5.2 add_convert_fusion.2
  289.7 31.5 %while.48 = (s32[]{:T(128)}, bf16[2,512,8,64]{1,3,2,0:T(8,128)(2,1)S(1)}, f32[2,8,512]{2,1,0:T(8,128)S(1)}, s32[2,512]{1,0:T(2,128)S(1)}, pred[2,512]{1,0:T(4,12...) while((s32[]{:T(128)}, ...), condition=%wide.region_5.6_spmd.clone, body=%wide.region_2.5_spmd.clone.sunk | while | flops 1125913600 | bytes 55724152 | solution.py:98
  290.9 4.9 fusion.155
  300.1 5.4 fusion.157
  306.7 4.9 fusion.155
  315.8 5.4 fusion.157
  322.1 191.8 %while.49 = (s32[]{:T(128)}, f32[1024,8,64]{0,2,1:T(8,128)}, f32[1024,8,64]{0,2,1:T(8,128)}, f32[2,512,8,64]{1,0,3,2:T(2,128)}, bf16[2,512,8,64]{1,3,2,0:T(8,128...) while((s32[]{:T(128)}, f32[1024,8,64]{0,2,1:T(8,128)}, ...), condition=%wide.region_9.10_spmd.clone, body=%wide.region_7.9_spmd.clone.sunk | while | flops 2746764288 | bytes 187764448 | solution.py:147
  323.6 9.4 subtract_exponential_fusion.3
  333.0 9.5 fusion.168
  342.5 22.1 %fusion.169 = f32[1,512,8,64]{1,3,2,0:T(8,128)S(1)} fusion(bf16[1024,8,64]{0,2,1:T(8,128)(2,1)} %get-tuple-element.563, f32[8,512,1024]{2,1,0:T(8,128)} %subtract_exponential_fusion.3, f32[8,512,1024]{2,1,0:T(8,128)} %fusion.168), kind=kOutput, calls=%fused_computation.45.clone.1 | convolution fusion | flops 557847552 | bytes 35651584 | tf_op jit(solution)/shard_map/while/body/eval_jaxpr/while/body/eval_jaxpr/hqk,khd->qhd/dot_general | solution.py:132
  365.7 19.6 %dynamic_update_slice.35 = f32[2,512,8,64]{1,0,3,2:T(2,128)} dynamic-update-slice(f32[2,512,8,64]{1,0,3,2:T(2,128)} %get-tuple-element.545, f32[1,512,8,64]{1,0,3,2:T(1,128)S(1)} %copy.64, s32[]{:T(128)} %get-tuple-element.542, s32[]{:T(128)} %constant.124.clone.1..sunk, s32[]{:T(128)} %constant.124.clone.1..sunk, s32[]{:T(128)} %constant.124.clone.1..sunk) | dynamic-update-slice | bytes 2097156 | tf_op jit(solution)/shard_map/while/body/eval_jaxpr/while/body/jit(dynamic_update_index_in_dim)/dynamic_update_slice | solution.py:147
  385.3 23.5 %bitcast_add_fusion.4 = f32[1024,8,64]{0,2,1:T(8,128)} fusion(f32[1024,8,64]{0,2,1:T(8,128)} %get-tuple-element.543, f32[8,512,1024]{2,1,0:T(8,128)} %subtract_exponential_fusion.3, f32[8,512,1024]{2,1,0:T(8,128)} %fusion.168, pred[]{:T(512)S(6)} %compare.7, bf16[2,512,8,64]{1,3,2,0:T(8,128)(2,1)} %get-tuple-element.560, s32[]{:T(128)} %get-tuple-element.542), kind=kOutput, calls=%fused_computation.43.clone.1 | convolution fusion | flops 558896128 | bytes 71827968 | tf_op jit(solution)/shard_map/while/body/eval_jaxpr/while/body/eval_jaxpr/hqk,qhd->khd/dot_general | solution.py:135
  408.8 7.8 bitcast_add_fusion.5
  419.1 9.5 subtract_exponential_fusion.3
  428.6 9.1 fusion.168
  437.8 22.1 %fusion.169 = f32[1,512,8,64]{1,3,2,0:T(8,128)S(1)} fusion(bf16[1024,8,64]{0,2,1:T(8,128)(2,1)} %get-tuple-element.563, f32[8,512,1024]{2,1,0:T(8,128)} %subtract_exponential_fusion.3, f32[8,512,1024]{2,1,0:T(8,128)} %fusion.168), kind=kOutput, calls=%fused_computation.45.clone.1 | convolution fusion | flops 557847552 | bytes 35651584 | tf_op jit(solution)/shard_map/while/body/eval_jaxpr/while/body/eval_jaxpr/hqk,khd->qhd/dot_general | solution.py:132
  460.9 19.6 %dynamic_update_slice.35 = f32[2,512,8,64]{1,0,3,2:T(2,128)} dynamic-update-slice(f32[2,512,8,64]{1,0,3,2:T(2,128)} %get-tuple-element.545, f32[1,512,8,64]{1,0,3,2:T(1,128)S(1)} %copy.64, s32[]{:T(128)} %get-tuple-element.542, s32[]{:T(128)} %constant.124.clone.1..sunk, s32[]{:T(128)} %constant.124.clone.1..sunk, s32[]{:T(128)} %constant.124.clone.1..sunk) | dynamic-update-slice | bytes 2097156 | tf_op jit(solution)/shard_map/while/body/eval_jaxpr/while/body/jit(dynamic_update_index_in_dim)/dynamic_update_slice | solution.py:147
  480.6 24.3 %bitcast_add_fusion.4 = f32[1024,8,64]{0,2,1:T(8,128)} fusion(f32[1024,8,64]{0,2,1:T(8,128)} %get-tuple-element.543, f32[8,512,1024]{2,1,0:T(8,128)} %subtract_exponential_fusion.3, f32[8,512,1024]{2,1,0:T(8,128)} %fusion.168, pred[]{:T(512)S(6)} %compare.7, bf16[2,512,8,64]{1,3,2,0:T(8,128)(2,1)} %get-tuple-element.560, s32[]{:T(128)} %get-tuple-element.542), kind=kOutput, calls=%fused_computation.43.clone.1 | convolution fusion | flops 558896128 | bytes 71827968 | tf_op jit(solution)/shard_map/while/body/eval_jaxpr/while/body/eval_jaxpr/hqk,qhd->khd/dot_general | solution.py:135
  504.9 7.8 bitcast_add_fusion.5
  526.6 6.1 convolution_convert_fusion.4
  533.5 6.0 convolution_convert_fusion.3
  545.8 7.7 fusion.95
  553.4 5.6 fusion.94
  559.1 14.5 %fusion.93 = f32[1024,2048]{1,0:T(8,128)} fusion(bf16[1024,2048]{1,0:T(8,128)(2,1)} %all-gather.9.cloned.1.call-done, bf16[2048,2048]{1,0:T(8,128)(2,1)} %all-gather.19.cloned.1.call-done), kind=kOutput, calls=%fused_computation.160 | convolution fusion | flops 8589934592 | bytes 20971520 | tf_op jit(solution)/shard_map/dot_general | solution.py:215
  573.6 18.8 %convert_reduce_fusion = (f32[2048]{0:T(1024)S(1)}, bf16[1024,2048]{1,0:T(8,128)(2,1)S(1)}) fusion(f32[1024,2048]{1,0:T(8,128)} %fusion.93, f32[2048]{0:T(1024)S(1)} %convert_element_type.197, bf16[1024,2048]{1,0:T(8,128)(2,1)} %all-gather.23.cloned.1.call-done, bf16[2048,2048]{1,0:T(8,128)(2,1)} %all-gather.21.cloned.1.call-done), kind=kOutput, calls=%fused_computation.83 | convolution fusion | flops 8638167040 | bytes 25182208 | tf_op jit(solution)/shard_map/dot_general | solution.py:57
  594.3 13.8 %fusion.96 = f32[1024,2048]{1,0:T(8,128)} fusion(bf16[1024,2048]{1,0:T(8,128)(2,1)S(1)} %get-tuple-element.338, bf16[2048,2048]{1,0:T(8,128)(2,1)} %all-gather.19.cloned.1.call-done), kind=kOutput, calls=%fused_computation.163 | convolution fusion | flops 8589934592 | bytes 20971520 | tf_op jit(solution)/shard_map/dot_general | solution.py:57
  608.1 11.4 add_convert_fusion
  619.6 16.1 %fusion.91 = f32[1024,2048]{1,0:T(8,128)S(1)} fusion(bf16[2048,2048]{1,0:T(8,128)(2,1)} %all-gather.21.cloned.1.call-done, f32[1024,2048]{1,0:T(8,128)} %fusion.93, f32[2048]{0:T(1024)S(1)} %convert_element_type.197), kind=kOutput, calls=%fused_computation.159 | convolution fusion | flops 8610906112 | bytes 25174016 | tf_op jit(solution)/shard_map/dot_general | solution.py:228
  640.1 14.1 %convolution_convert_fusion.1 = bf16[2048,2048]{1,0:T(8,128)(2,1)} fusion(bf16[1024,2048]{1,0:T(8,128)(2,1)} %all-gather.9.cloned.1.call-done, bf16[1024,2048]{1,0:T(8,128)(2,1)} %copy-done.38), kind=kOutput, calls=%fused_computation.88 | convolution fusion | flops 8594128896 | bytes 16777216 | tf_op jit(solution)/shard_map/dot_general | solution.py:63
  654.3 16.1 %convolution_convert_fusion = bf16[2048,2048]{1,0:T(8,128)(2,1)} fusion(bf16[1024,2048]{1,0:T(8,128)(2,1)} %all-gather.23.cloned.1.call-done, f32[1024,2048]{1,0:T(8,128)} %fusion.93, f32[2048]{0:T(1024)S(1)} %convert_element_type.197), kind=kOutput, calls=%fused_computation.87 | convolution fusion | flops 8615100416 | bytes 20979712 | tf_op jit(solution)/shard_map/dot_general | solution.py:63
  678.7 69.7 %reduce-scatter.17.cloned.1.call-done = bf16[256,512]{1,0:T(8,128)(2,1)} async-done(((bf16[2048,512]{1,0:T(8,128)(2,1)}), bf16[256,512]{1,0:T(8,128)(2,1)}) %reduce-scatter.17.cloned.1.call-update) | async-done | bytes 262160 | tf_op jit(solution)/shard_map/reduce_scatter | solution.py:278
  750.2 69.5 %reduce-scatter.19.cloned.1.call-done = bf16[512,256]{1,0:T(8,128)(2,1)} async-done(((bf16[512,2048]{1,0:T(8,128)(2,1)}), bf16[512,256]{1,0:T(8,128)(2,1)}) %reduce-scatter.19.cloned.1.call-update) | async-done | bytes 262160 | tf_op jit(solution)/shard_map/reduce_scatter | solution.py:292
  821.5 35.3 %all-reduce.1 = (f32[512]{0:T(512)}, f32[512]{0:T(512)}, f32[512]{0:T(512)}, f32[2048]{0:T(1024)}) all-reduce(f32[512]{0:T(512)S(1)} %reduce_sum.130, f32[512]{0:T(512)S(1)} %reduce_sum.132, f32[512]{0:T(512)S(1)} %reduce_sum.134, f32[2048]{0:T(1024)S(1)} %get-tuple-element.337), channel_id=1, replica_groups=mesh['dp'=8,'tensor'=4] {'dp'}, use_global_device_ids=true, to_apply=%region_19.20 | all-reduce | flops 3584 | bytes 28672 | tf_op jit(solution)/shard_map/psum | solution.py:305
  856.8 9.1 reduce-scatter.11.cloned.1.call-done
  868.2 44.7 %reduce-scatter.9.cloned.1.call-done = bf16[256,2048]{1,0:T(8,128)(2,1)} async-done(((bf16[1024,2048]{1,0:T(8,128)(2,1)}), bf16[256,2048]{1,0:T(8,128)(2,1)}) %reduce-scatter.9.cloned.1.call-update) | async-done | bytes 1048592 | tf_op jit(solution)/shard_map/reduce_scatter | solution.py:231
  912.9 4.5 convert_reduce_fusion.3
  917.4 43.0 %all-reduce = (f32[2048]{0:T(1024)}, f32[2048]{0:T(1024)}, f32[2048]{0:T(1024)S(1)}) all-reduce(f32[2048]{0:T(1024)S(1)} %get-tuple-element.284, f32[2048]{0:T(1024)S(1)} %get-tuple-element.287, f32[2048]{0:T(1024)S(1)} %get-tuple-element.355), channel_id=1, replica_groups=mesh['dp'=8,'tensor'=4] {'dp','tensor'}, use_global_device_ids=true, to_apply=%region_14.15 | all-reduce | flops 6144 | bytes 49152 | tf_op jit(solution)/shard_map/psum | solution.py:321
  960.4 104.5 %reduce-scatter.21.cloned.1.call-done = bf16[256,2048]{1,0:T(8,128)(2,1)} async-done(((bf16[2048,2048]{1,0:T(8,128)(2,1)}), bf16[256,2048]{1,0:T(8,128)(2,1)}) %reduce-scatter.21.cloned.1.call-update) | async-done | bytes 1048592 | tf_op jit(solution)/shard_map/reduce_scatter | solution.py:284
  1067.7 147.7 %reduce-scatter.23.cloned.1.call-done = bf16[2048,256]{1,0:T(8,128)(2,1)} async-done(((bf16[2048,2048]{1,0:T(8,128)(2,1)}), bf16[2048,256]{1,0:T(8,128)(2,1)}) %reduce-scatter.23.cloned.1.call-update) | async-done | bytes 1048592 | tf_op jit(solution)/shard_map/reduce_scatter | solution.py:298
  (204 shorter events, 91.3 us)
Async XLA Ops:
  7.2 54.8 %all-gather.11.cloned.1.call-start = ((), (), s32[]{:S(2)}) async-start(), calls=%async_computation.9 | async-start | bytes 2359296 | tf_op jit(solution)/shard_map/all_gather | solution.py:196
  7.9 89.2 %all-gather.9.cloned.1.call-start = ((), (), s32[]{:S(2)}) async-start(), calls=%async_computation.8 | async-start | bytes 5242880 | tf_op jit(solution)/shard_map/all_gather | solution.py:194
  8.7 3.9 copy-start.18
  10.8 9.1 copy-start.31
  10.8 9.1 copy-start.32
  10.8 9.8 copy-start.33
  10.8 1.7 copy-start.20
  15.8 132.6 %all-gather.13.cloned.1.call-start = ((), (), s32[]{:S(2)}) async-start(), calls=%async_computation.10 | async-start | bytes 2359296 | tf_op jit(solution)/shard_map/all_gather | solution.py:197
  16.5 182.7 %all-gather.17.cloned.1.call-start = ((), (), s32[]{:S(2)}) async-start(), calls=%async_computation.12 | async-start | bytes 2359296 | tf_op jit(solution)/shard_map/all_gather | solution.py:202
  17.1 216.2 %all-gather.23.cloned.1.call-start = ((), (), s32[]{:S(2)}) async-start(), calls=%async_computation.16 | async-start | bytes 5242880 | tf_op jit(solution)/shard_map/all_gather | solution.py:236
  17.7 266.8 %all-gather.15.cloned.1.call-start = ((), (), s32[]{:S(2)}) async-start(), calls=%async_computation.11 | async-start | bytes 2359296 | tf_op jit(solution)/shard_map/all_gather | solution.py:198
  18.2 540.8 %all-gather.19.cloned.1.call-start = ((), (), s32[]{:S(2)}) async-start(), calls=%async_computation.13 | async-start | bytes 9437184 | tf_op jit(solution)/shard_map/all_gather | solution.py:199
  19.0 554.6 %all-gather.21.cloned.1.call-start = ((), (), s32[]{:S(2)}) async-start(), calls=%async_computation.14 | async-start | bytes 9437184 | tf_op jit(solution)/shard_map/all_gather | solution.py:203
  19.7 651.6 %reduce-scatter.13.cloned.1.call-start = ((), (), s32[]{:S(2)}) async-start(), calls=%async_computation.18 | async-start | bytes 2359296 | tf_op jit(solution)/shard_map/reduce_scatter | solution.py:266
  20.9 132.8 %copy-start.13 = (f32[1024,16]{0,1:T(8,128)}, f32[1024,16]{0,1:T(8,128)S(1)}, u32[]{:S(2)}) copy-start(f32[1024,16]{0,1:T(8,128)S(1)} %get-tuple-element.362) | copy-start | bytes 196612
  20.9 132.8 %copy-start.15 = (f32[1024,16]{0,1:T(8,128)}, f32[1024,16]{0,1:T(8,128)S(1)}, u32[]{:S(2)}) copy-start(f32[1024,16]{0,1:T(8,128)S(1)} %get-tuple-element.363) | copy-start | bytes 196612
  239.5 5.2 copy-start.9
  248.4 41.3 %copy-start.6 = (bf16[2,512,8,64]{1,3,2,0:T(8,128)(2,1)S(1)}, bf16[2,512,8,64]{1,3,2,0:T(8,128)(2,1)}, u32[]{:S(2)}) copy-start(bf16[2,512,8,64]{1,3,2,0:T(8,128)(2,1)} %custom-call.3) | copy-start | bytes 3145732
  248.4 41.3 %copy-start.17 = (f32[2,8,512]{2,1,0:T(8,128)S(1)}, f32[2,8,512]{2,1,0:T(8,128)}, u32[]{:S(2)}) copy-start(f32[2,8,512]{2,1,0:T(8,128)} %custom-call.4) | copy-start | bytes 98308
  385.3 23.5 %copy-start = (f32[1024,8,64]{0,2,1:T(8,128)S(1)}, f32[1024,8,64]{0,2,1:T(8,128)}, u32[]{:S(2)}) copy-start(f32[1024,8,64]{0,2,1:T(8,128)} %get-tuple-element.544) | copy-start | bytes 6291460 | tf_op jit(solution)/shard_map/while/body/eval_jaxpr/while
  416.6 1.3 copy-start.1
  480.6 24.3 %copy-start = (f32[1024,8,64]{0,2,1:T(8,128)S(1)}, f32[1024,8,64]{0,2,1:T(8,128)}, u32[]{:S(2)}) copy-start(f32[1024,8,64]{0,2,1:T(8,128)} %get-tuple-element.544) | copy-start | bytes 6291460 | tf_op jit(solution)/shard_map/while/body/eval_jaxpr/while
  514.0 5.1 copy-start.14
  514.0 5.1 copy-start.16
  517.6 5.0 copy-start.34
  521.7 4.9 copy-start.12
  526.5 150.4 %reduce-scatter.15.cloned.1.call-start = ((), (), s32[]{:S(2)}) async-start(), calls=%async_computation.19 | async-start | bytes 2359296 | tf_op jit(solution)/shard_map/reduce_scatter | solution.py:272
  526.5 6.1 copy-start.2
  532.6 215.8 %reduce-scatter.17.cloned.1.call-start = ((), (), s32[]{:S(2)}) async-start(), calls=%async_computation.20 | async-start | bytes 2359296 | tf_op jit(solution)/shard_map/reduce_scatter | solution.py:278
  533.5 6.1 copy-start.28
  533.5 6.1 copy-start.8
  539.5 280.2 %reduce-scatter.19.cloned.1.call-start = ((), (), s32[]{:S(2)}) async-start(), calls=%async_computation.21 | async-start | bytes 2359296 | tf_op jit(solution)/shard_map/reduce_scatter | solution.py:292
  539.6 2.2 copy-start.35
  545.5 320.4 %reduce-scatter.11.cloned.1.call-start = ((), (), s32[]{:S(2)}) async-start(), calls=%async_computation.17 | async-start | bytes 5242880 | tf_op jit(solution)/shard_map/reduce_scatter | solution.py:262
  545.7 7.7 copy-start.11
  545.7 7.7 copy-start.36
  592.4 1.9 copy-start.38
  594.3 13.8 %copy-start.4 = (f32[1024,2048]{1,0:T(8,128)S(1)}, f32[1024,2048]{1,0:T(8,128)}, u32[]{:S(2)}) copy-start(f32[1024,2048]{1,0:T(8,128)} %fusion.94) | copy-start | bytes 25165828
  619.5 293.4 %reduce-scatter.9.cloned.1.call-start = ((), (), s32[]{:S(2)}) async-start(), calls=%async_computation.15 | async-start | bytes 5242880 | tf_op jit(solution)/shard_map/reduce_scatter | solution.py:231
  619.6 16.1 %copy-start.37 = (bf16[512,2048]{1,0:T(8,128)(2,1)S(1)}, bf16[512,2048]{1,0:T(8,128)(2,1)}, u32[]{:S(2)}) copy-start(bf16[512,2048]{1,0:T(8,128)(2,1)} %all-gather.17.cloned.1.call-done) | copy-start | bytes 6291460
  640.1 424.8 %reduce-scatter.21.cloned.1.call-start = ((), (), s32[]{:S(2)}) async-start(), calls=%async_computation.22 | async-start | bytes 9437184 | tf_op jit(solution)/shard_map/reduce_scatter | solution.py:284
  654.3 561.1 %reduce-scatter.23.cloned.1.call-start = ((), (), s32[]{:S(2)}) async-start(), calls=%async_computation.23 | async-start | bytes 9437184 | tf_op jit(solution)/shard_map/reduce_scatter | solution.py:298
  670.4 195.4 %copy-start.3 = (bf16[256,2048]{1,0:T(8,128)(2,1)S(1)}, bf16[256,2048]{1,0:T(8,128)(2,1)}, u32[]{:S(2)}) copy-start(bf16[256,2048]{1,0:T(8,128)(2,1)} %param.21) | copy-start | bytes 3145732
  670.5 195.4 %copy-start.19 = (f32[2048]{0:T(1024)S(1)}, f32[2048]{0:T(1024)}, u32[]{:S(2)}) copy-start(f32[2048]{0:T(1024)} %copy-done.18) | copy-start | bytes 24580
  670.5 195.4 %copy-start.21 = (f32[256]{0:T(256)S(1)}, f32[256]{0:T(256)}, u32[]{:S(2)}) copy-start(f32[256]{0:T(256)} %copy-done.20) | copy-start | bytes 3076
  670.5 195.4 %copy-start.26 = (f32[256]{0:T(256)S(1)}, f32[256]{0:T(256)}, u32[]{:S(2)}) copy-start(f32[256]{0:T(256)} %copy-done.25) | copy-start | bytes 3076
  671.1 241.8 %copy-start.5 = (bf16[256,2048]{1,0:T(8,128)(2,1)S(1)}, bf16[256,2048]{1,0:T(8,128)(2,1)}, u32[]{:S(2)}) copy-start(bf16[256,2048]{1,0:T(8,128)(2,1)} %param.37) | copy-start | bytes 3145732
  960.4 258.3 %copy-start.27 = (f32[2048]{0:T(1024)}, f32[2048]{0:T(1024)S(1)}, u32[]{:S(2)}) copy-start(f32[2048]{0:T(1024)S(1)} %get-tuple-element.601) | copy-start | bytes 24580
  (9 other events, 7.6 us)
Sparse Core Ops, SparseCore 0:
  10.1 51.8 all-gather.10
  64.1 32.9 all-gather.8
  99.2 49.0 all-gather.12
  150.3 48.8 all-gather.16
  200.6 32.6 all-gather.22
  235.2 49.1 all-gather.14
  286.5 122.9 all-gather.18
  411.6 123.1 all-gather.20
  538.9 66.6 reduce-scatter.12
  609.5 67.3 reduce-scatter.14
  681.0 67.3 reduce-scatter.16
  751.8 67.9 reduce-scatter.18
  822.3 43.5 reduce-scatter.10
  868.3 44.5 reduce-scatter.8
  916.3 148.5 reduce-scatter.20
  1068.4 146.9 reduce-scatter.22
where the time goes:
time: 1240 us; the launch traced here: 1230 us
  waiting for transfers between devices  687 us (55%)
  matrix products  330 us (27%)
  blocking collectives  78.3 us (6%)
  local copies, waits for them, and re-layouts  67.5 us (5%)
  other arithmetic  46.7 us (4%)
  between operations  15.4 us (1%)
    reduce_scatter x1, waiting for transfers between devices, on_device(): lax.psum_scatter(contract_first(activated, cot_all).astype(jnp.bfloat16),...  148 us
    reduce_scatter x1, waiting for transfers between devices, on_device(): lax.psum_scatter(contract_first(normed_all, grad_hidden).astype(jnp.bfloa...  104 us
    reduce_scatter x1, waiting for transfers between devices, on_device(): lax.psum_scatter(contract_first(normed_all, grad_v).astype(jnp.bfloat16),...  69.7 us
    reduce_scatter x1, waiting for transfers between devices, on_device(): lax.psum_scatter(contract_first(attended_flat, cot_all).astype(jnp.bfloat...  69.5 us
    dot_general x6, matrix products, contract_last(): lax.dot_general(left, right, (((1,), (1,)), ((), ())), preferred_element_...  63.5 us
    dot_general x6, matrix products, contract_first(): lax.dot_general(left, right, (((0,), (0,)), ((), ())), preferred_element_...  49.8 us
    dot_general x2, matrix products, one_block(): jnp.einsum('hqk,qhd->khd', grad_scores, query_rows, preferred_element_typ...  47.7 us
    all_gather x1, waiting for transfers between devices, on_device(): lax.all_gather(key_weight, 'dp', axis=0, tiled=True)  45.9 us
  transfers between devices with their start and end apart: 16, of which 13 were waited for; matrix products, arithmetic and copies ran while one was open for 35% of the time, Pallas kernels for 0%

commit v1 on v0

--- a/solution.py
+++ b/solution.py
@@ -191,7 +191,27 @@
     inv_scale = lax.rsqrt(jnp.mean(centred * centred, -1, keepdims=True) + EPS)
     standard = centred * inv_scale
     normed = (standard * gain_wide + norm_bias.astype(jnp.float32)).astype(jnp.bfloat16)
-    normed_all = lax.all_gather(normed, "tensor", axis=0, tiled=True)
+    after = lax.psum(1, axis_name="tensor")
+    fresh = lax.axis_index("tensor")
+    block_now, r_now, vec_out = (after, fresh, normed.shape[0])
+    ledger = [(src_i, (src_i + 1) % block_now) for src_i in range(block_now)]
+    rack = [(src_i, (src_i - 1) % block_now) for src_i in range(block_now)]
+    normed_all = jnp.zeros(
+        (*normed.shape[:0], block_now * vec_out, *normed.shape[1:]), normed.dtype
+    )
+    normed_all = lax.dynamic_update_slice_in_dim(normed_all, normed, r_now * vec_out, axis=0)
+    v_next = v1 = normed
+    u1 = block_now // 2
+    for kk in range(1, u1 + 1):
+        v_next = lax.ppermute(v_next, axis_name="tensor", perm=ledger)
+        normed_all = lax.dynamic_update_slice_in_dim(
+            normed_all, v_next, (r_now - kk) % block_now * vec_out, axis=0
+        )
+        if kk < block_now - u1:
+            v1 = lax.ppermute(v1, axis_name="tensor", perm=rack)
+            normed_all = lax.dynamic_update_slice_in_dim(
+                normed_all, v1, (r_now + kk) % block_now * vec_out, axis=0
+            )
     full_query, full_key, full_value, full_up = (
         lax.all_gather(query_weight, "dp", axis=0, tiled=True),
         lax.all_gather(key_weight, "dp", axis=0, tiled=True),

time: 1240 us -> 1200 us (0.968)
  waiting for transfers between devices: 687 us -> 646 us
    all_gather x1, waiting for transfers between devices: 45.9 us -> 5.67 us  [on_device(): lax.all_gather(key_weight, 'dp', axis=0, tiled=True)]
    all_gather x1 -> x0, waiting for transfers between devices: 35.1 us -> none  [on_device(): normed_all = lax.all_gather(normed, 'tensor', axis=0, tiled=True)]
    ppermute x0 -> x3, waiting for transfers between devices: none -> 29.4 us  [the longest x2 29.4 us: on_device(): v_next = lax.ppermute(v_next, axis_name='tensor', perm=ledger)]
    all_gather x1, waiting for transfers between devices: 41.2 us -> 14.3 us  [on_device(): lax.all_gather(output_weight, 'dp', axis=1, tiled=True)]
    reduce_scatter x1, waiting for transfers between devices: 3.65 us -> 29 us  [on_device(): lax.psum_scatter(contract_first(normed_all, grad_k).astype(jnp.bfloat16),...]
  transfers between devices with their start and end apart: 16 -> 18, of which waited for: 13 -> 14; matrix products, arithmetic and copies ran while one was open for 35% -> 36% of each run, Pallas kernels for 0% -> 0%
where the time goes in v1:
time: 1200 us; the launch traced here: 1190 us
  waiting for transfers between devices  646 us (54%)
  matrix products  332 us (28%)
  blocking collectives  78.3 us (7%)
  local copies, waits for them, and re-layouts  69 us (6%)
  other arithmetic  41.5 us (3%)
  between operations  15.5 us (1%)
    reduce_scatter x1, waiting for transfers between devices, on_device(): lax.psum_scatter(contract_first(activated, cot_all).astype(jnp.bfloat16),...  148 us
    reduce_scatter x1, waiting for transfers between devices, on_device(): lax.psum_scatter(contract_first(normed_all, grad_hidden).astype(jnp.bfloa...  104 us
    reduce_scatter x1, waiting for transfers between devices, on_device(): lax.psum_scatter(contract_first(attended_flat, cot_all).astype(jnp.bfloat...  69.7 us
    reduce_scatter x1, waiting for transfers between devices, on_device(): lax.psum_scatter(contract_first(normed_all, grad_v).astype(jnp.bfloat16),...  69.5 us
    dot_general x6, matrix products, contract_last(): lax.dot_general(left, right, (((1,), (1,)), ((), ())), preferred_element_...  63.6 us
    dot_general x6, matrix products, contract_first(): lax.dot_general(left, right, (((0,), (0,)), ((), ())), preferred_element_...  50.1 us
    dot_general x2, matrix products, one_block(): jnp.einsum('hqk,qhd->khd', grad_scores, query_rows, preferred_element_typ...  48.7 us
    dot_general x2, matrix products, one_block(): jnp.einsum('hqk,khd->qhd', grad_scores, keys_rot, preferred_element_type=...  45 us
  transfers between devices with their start and end apart: 18, of which 14 were waited for; matrix products, arithmetic and copies ran while one was open for 36% of the time, Pallas kernels for 0%

profile of v1, /device:TPU:0, one launch (start us, length us, event | category | flops | bytes accessed | tf_op | source)
XLA Modules:
  0.0 1188.8 jit_solution(17435784464138922135)
XLA Ops:
  20.8 20.2 %collective-permute-done = bf16[256,2048]{1,0:T(8,128)(2,1)S(1)} collective-permute-done((bf16[256,2048]{1,0:T(8,128)(2,1)S(1)}, bf16[256,2048]{1,0:T(8,128)(2,1)S(1)}, u32[]{:S(2)}, u32[]{:S(2)}) %collective-permute-start) | collective-permute-done | bytes 1048608 | tf_op jit(solution)/shard_map/ppermute | solution.py:206
  46.1 9.2 collective-permute-done.2
  56.3 5.7 all-gather.10.cloned.1.call-done
  62.0 5.2 convolution_add_fusion
  68.6 43.1 %all-gather.8.cloned.1.call-done = bf16[2048,512]{1,0:T(8,128)(2,1)} async-done(((bf16[256,512]{1,0:T(8,128)(2,1)}), bf16[2048,512]{1,0:T(8,128)(2,1)}) %all-gather.8.cloned.1.call-update) | async-done | bytes 2097168 | tf_op jit(solution)/shard_map/all_gather | solution.py:216
  111.7 5.4 convolution_add_fusion.1
  119.5 42.0 %all-gather.12.cloned.1.call-done = bf16[2048,512]{1,0:T(8,128)(2,1)} async-done(((bf16[256,512]{1,0:T(8,128)(2,1)}), bf16[2048,512]{1,0:T(8,128)(2,1)}) %all-gather.12.cloned.1.call-update) | async-done | bytes 2097168 | tf_op jit(solution)/shard_map/all_gather | solution.py:218
  161.5 5.2 add_convert_fusion.2
  166.8 31.3 %while.48 = (s32[]{:T(128)}, bf16[2,512,8,64]{1,3,2,0:T(8,128)(2,1)S(1)}, f32[2,8,512]{2,1,0:T(8,128)S(1)}, s32[2,512]{1,0:T(2,128)S(1)}, pred[2,512]{1,0:T(4,12...) while((s32[]{:T(128)}, ...), condition=%wide.region_5.6_spmd.clone, body=%wide.region_2.5_spmd.clone.sunk | while | flops 1125913600 | bytes 55723644 | solution.py:98
  168.2 4.7 fusion.156
  177.2 5.4 fusion.158
  192.7 5.4 fusion.158
  198.1 14.3 %all-gather.14.cloned.1.call-done = bf16[512,2048]{1,0:T(8,128)(2,1)} async-done(((bf16[512,256]{1,0:T(8,128)(2,1)}), bf16[512,2048]{1,0:T(8,128)(2,1)}) %all-gather.14.cloned.1.call-update) | async-done | bytes 2097168 | tf_op jit(solution)/shard_map/all_gather | solution.py:222
  212.4 34.0 %all-gather.20.cloned.1.call-done = bf16[1024,2048]{1,0:T(8,128)(2,1)} async-done(((bf16[256,2048]{1,0:T(8,128)(2,1)}), bf16[1024,2048]{1,0:T(8,128)(2,1)}) %all-gather.20.cloned.1.call-update) | async-done | bytes 4194320 | tf_op jit(solution)/shard_map/all_gather | solution.py:256
  246.4 6.2 convolution_convert_fusion.6
  257.7 193.8 %while.49 = (s32[]{:T(128)}, f32[1024,8,64]{0,2,1:T(8,128)}, f32[1024,8,64]{0,2,1:T(8,128)}, f32[2,512,8,64]{1,0,3,2:T(2,128)}, bf16[2,512,8,64]{1,3,2,0:T(8,128...) while((s32[]{:T(128)}, f32[1024,8,64]{0,2,1:T(8,128)}, ...), condition=%wide.region_9.10_spmd.clone, body=%wide.region_7.9_spmd.clone.sunk | while | flops 2746764288 | bytes 187764448 | solution.py:147
  259.1 9.5 subtract_exponential_fusion.3
  268.6 9.2 fusion.169
  277.8 22.0 %fusion.170 = f32[1,512,8,64]{1,3,2,0:T(8,128)S(1)} fusion(bf16[1024,8,64]{0,2,1:T(8,128)(2,1)} %get-tuple-element.565, f32[8,512,1024]{2,1,0:T(8,128)} %subtract_exponential_fusion.3, f32[8,512,1024]{2,1,0:T(8,128)} %fusion.169), kind=kOutput, calls=%fused_computation.45.clone.1 | convolution fusion | flops 557847552 | bytes 35651584 | tf_op jit(solution)/shard_map/while/body/eval_jaxpr/while/body/eval_jaxpr/hqk,khd->qhd/dot_general | solution.py:132
  300.9 19.6 %dynamic_update_slice.55 = f32[2,512,8,64]{1,0,3,2:T(2,128)} dynamic-update-slice(f32[2,512,8,64]{1,0,3,2:T(2,128)} %get-tuple-element.547, f32[1,512,8,64]{1,0,3,2:T(1,128)S(1)} %copy.64, s32[]{:T(128)} %get-tuple-element.544, s32[]{:T(128)} %constant.152.clone.1..sunk, s32[]{:T(128)} %constant.152.clone.1..sunk, s32[]{:T(128)} %constant.152.clone.1..sunk) | dynamic-update-slice | bytes 2097156 | tf_op jit(solution)/shard_map/while/body/eval_jaxpr/while/body/jit(dynamic_update_index_in_dim)/dynamic_update_slice | solution.py:147
  320.5 23.6 %bitcast_add_fusion.4 = f32[1024,8,64]{0,2,1:T(8,128)} fusion(f32[1024,8,64]{0,2,1:T(8,128)} %get-tuple-element.545, f32[8,512,1024]{2,1,0:T(8,128)} %subtract_exponential_fusion.3, f32[8,512,1024]{2,1,0:T(8,128)} %fusion.169, pred[]{:T(512)S(6)} %compare.10, bf16[2,512,8,64]{1,3,2,0:T(8,128)(2,1)} %get-tuple-element.562, s32[]{:T(128)} %get-tuple-element.544), kind=kOutput, calls=%fused_computation.43.clone.1 | convolution fusion | flops 558896128 | bytes 71827968 | tf_op jit(solution)/shard_map/while/body/eval_jaxpr/while/body/eval_jaxpr/hqk,qhd->khd/dot_general | solution.py:135
  344.1 8.1 bitcast_add_fusion.5
  354.8 9.5 subtract_exponential_fusion.3
  364.3 9.2 fusion.169
  373.5 23.0 %fusion.170 = f32[1,512,8,64]{1,3,2,0:T(8,128)S(1)} fusion(bf16[1024,8,64]{0,2,1:T(8,128)(2,1)} %get-tuple-element.565, f32[8,512,1024]{2,1,0:T(8,128)} %subtract_exponential_fusion.3, f32[8,512,1024]{2,1,0:T(8,128)} %fusion.169), kind=kOutput, calls=%fused_computation.45.clone.1 | convolution fusion | flops 557847552 | bytes 35651584 | tf_op jit(solution)/shard_map/while/body/eval_jaxpr/while/body/eval_jaxpr/hqk,khd->qhd/dot_general | solution.py:132
  397.5 19.6 %dynamic_update_slice.55 = f32[2,512,8,64]{1,0,3,2:T(2,128)} dynamic-update-slice(f32[2,512,8,64]{1,0,3,2:T(2,128)} %get-tuple-element.547, f32[1,512,8,64]{1,0,3,2:T(1,128)S(1)} %copy.64, s32[]{:T(128)} %get-tuple-element.544, s32[]{:T(128)} %constant.152.clone.1..sunk, s32[]{:T(128)} %constant.152.clone.1..sunk, s32[]{:T(128)} %constant.152.clone.1..sunk) | dynamic-update-slice | bytes 2097156 | tf_op jit(solution)/shard_map/while/body/eval_jaxpr/while/body/jit(dynamic_update_index_in_dim)/dynamic_update_slice | solution.py:147
  417.1 25.1 %bitcast_add_fusion.4 = f32[1024,8,64]{0,2,1:T(8,128)} fusion(f32[1024,8,64]{0,2,1:T(8,128)} %get-tuple-element.545, f32[8,512,1024]{2,1,0:T(8,128)} %subtract_exponential_fusion.3, f32[8,512,1024]{2,1,0:T(8,128)} %fusion.169, pred[]{:T(512)S(6)} %compare.10, bf16[2,512,8,64]{1,3,2,0:T(8,128)(2,1)} %get-tuple-element.562, s32[]{:T(128)} %get-tuple-element.544), kind=kOutput, calls=%fused_computation.43.clone.1 | convolution fusion | flops 558896128 | bytes 71827968 | tf_op jit(solution)/shard_map/while/body/eval_jaxpr/while/body/eval_jaxpr/hqk,qhd->khd/dot_general | solution.py:135
  442.2 7.9 bitcast_add_fusion.5
  464.0 6.1 convolution_convert_fusion.4
  471.0 6.0 convolution_convert_fusion.3
  483.3 7.7 fusion.96
  491.0 5.6 fusion.95
  496.6 14.5 %fusion.94 = f32[1024,2048]{1,0:T(8,128)} fusion(bf16[1024,2048]{1,0:T(8,128)(2,1)} %constant_dynamic-update-slice_fusion, bf16[2048,2048]{1,0:T(8,128)(2,1)} %all-gather.16.cloned.1.call-done), kind=kOutput, calls=%fused_computation.164 | convolution fusion | flops 8589934592 | bytes 20971520 | tf_op jit(solution)/shard_map/dot_general | solution.py:235
  511.1 18.7 %convert_reduce_fusion = (f32[2048]{0:T(1024)S(1)}, bf16[1024,2048]{1,0:T(8,128)(2,1)S(1)}) fusion(f32[1024,2048]{1,0:T(8,128)} %fusion.94, f32[2048]{0:T(1024)S(1)} %convert_element_type.197, bf16[1024,2048]{1,0:T(8,128)(2,1)} %all-gather.20.cloned.1.call-done, bf16[2048,2048]{1,0:T(8,128)(2,1)} %all-gather.18.cloned.1.call-done), kind=kOutput, calls=%fused_computation.83 | convolution fusion | flops 8638167040 | bytes 25182208 | tf_op jit(solution)/shard_map/dot_general | solution.py:57
  531.8 14.0 %fusion.97 = f32[1024,2048]{1,0:T(8,128)} fusion(bf16[1024,2048]{1,0:T(8,128)(2,1)S(1)} %get-tuple-element.338, bf16[2048,2048]{1,0:T(8,128)(2,1)} %all-gather.16.cloned.1.call-done), kind=kOutput, calls=%fused_computation.167 | convolution fusion | flops 8589934592 | bytes 20971520 | tf_op jit(solution)/shard_map/dot_general | solution.py:57
  545.8 11.4 add_convert_fusion
  557.3 16.1 %fusion.91 = f32[1024,2048]{1,0:T(8,128)S(1)} fusion(bf16[2048,2048]{1,0:T(8,128)(2,1)} %all-gather.18.cloned.1.call-done, f32[1024,2048]{1,0:T(8,128)} %fusion.94, f32[2048]{0:T(1024)S(1)} %convert_element_type.197), kind=kOutput, calls=%fused_computation.163 | convolution fusion | flops 8610906112 | bytes 25174016 | tf_op jit(solution)/shard_map/dot_general | solution.py:248
  577.9 14.2 %convolution_convert_fusion.1 = bf16[2048,2048]{1,0:T(8,128)(2,1)} fusion(bf16[1024,2048]{1,0:T(8,128)(2,1)} %constant_dynamic-update-slice_fusion, bf16[1024,2048]{1,0:T(8,128)(2,1)} %copy-done.42), kind=kOutput, calls=%fused_computation.88 | convolution fusion | flops 8594128896 | bytes 16777216 | tf_op jit(solution)/shard_map/dot_general | solution.py:63
  592.2 16.3 %convolution_convert_fusion = bf16[2048,2048]{1,0:T(8,128)(2,1)} fusion(bf16[1024,2048]{1,0:T(8,128)(2,1)} %all-gather.20.cloned.1.call-done, f32[1024,2048]{1,0:T(8,128)} %fusion.94, f32[2048]{0:T(1024)S(1)} %convert_element_type.197), kind=kOutput, calls=%fused_computation.87 | convolution fusion | flops 8615100416 | bytes 20979712 | tf_op jit(solution)/shard_map/dot_general | solution.py:63
  611.3 29.0 %reduce-scatter.15.cloned.1.call-done = bf16[256,512]{1,0:T(8,128)(2,1)} async-done(((bf16[2048,512]{1,0:T(8,128)(2,1)}), bf16[256,512]{1,0:T(8,128)(2,1)}) %reduce-scatter.15.cloned.1.call-update) | async-done | bytes 262160 | tf_op jit(solution)/shard_map/reduce_scatter | solution.py:292
  642.1 69.5 %reduce-scatter.17.cloned.1.call-done = bf16[256,512]{1,0:T(8,128)(2,1)} async-done(((bf16[2048,512]{1,0:T(8,128)(2,1)}), bf16[256,512]{1,0:T(8,128)(2,1)}) %reduce-scatter.17.cloned.1.call-update) | async-done | bytes 262160 | tf_op jit(solution)/shard_map/reduce_scatter | solution.py:298
  713.4 69.7 %reduce-scatter.19.cloned.1.call-done = bf16[512,256]{1,0:T(8,128)(2,1)} async-done(((bf16[512,2048]{1,0:T(8,128)(2,1)}), bf16[512,256]{1,0:T(8,128)(2,1)}) %reduce-scatter.19.cloned.1.call-update) | async-done | bytes 262160 | tf_op jit(solution)/shard_map/reduce_scatter | solution.py:312
  784.9 35.3 %all-reduce.1 = (f32[512]{0:T(512)}, f32[512]{0:T(512)}, f32[512]{0:T(512)}, f32[2048]{0:T(1024)}) all-reduce(f32[512]{0:T(512)S(1)} %reduce_sum.130, f32[512]{0:T(512)S(1)} %reduce_sum.132, f32[512]{0:T(512)S(1)} %reduce_sum.134, f32[2048]{0:T(1024)S(1)} %get-tuple-element.337), channel_id=1, replica_groups=mesh['dp'=8,'tensor'=4] {'dp'}, use_global_device_ids=true, to_apply=%region_19.20 | all-reduce | flops 3584 | bytes 28672 | tf_op jit(solution)/shard_map/psum | solution.py:325
  820.2 8.9 reduce-scatter.11.cloned.1.call-done
  831.4 44.8 %reduce-scatter.9.cloned.1.call-done = bf16[256,2048]{1,0:T(8,128)(2,1)} async-done(((bf16[1024,2048]{1,0:T(8,128)(2,1)}), bf16[256,2048]{1,0:T(8,128)(2,1)}) %reduce-scatter.9.cloned.1.call-update) | async-done | bytes 1048592 | tf_op jit(solution)/shard_map/reduce_scatter | solution.py:251
  880.8 43.0 %all-reduce = (f32[2048]{0:T(1024)}, f32[2048]{0:T(1024)}, f32[2048]{0:T(1024)S(1)}) all-reduce(f32[2048]{0:T(1024)S(1)} %get-tuple-element.284, f32[2048]{0:T(1024)S(1)} %get-tuple-element.287, f32[2048]{0:T(1024)S(1)} %get-tuple-element.357), channel_id=1, replica_groups=mesh['dp'=8,'tensor'=4] {'dp','tensor'}, use_global_device_ids=true, to_apply=%region_14.15 | all-reduce | flops 6144 | bytes 49152 | tf_op jit(solution)/shard_map/psum | solution.py:341
  923.8 104.5 %reduce-scatter.21.cloned.1.call-done = bf16[256,2048]{1,0:T(8,128)(2,1)} async-done(((bf16[2048,2048]{1,0:T(8,128)(2,1)}), bf16[256,2048]{1,0:T(8,128)(2,1)}) %reduce-scatter.21.cloned.1.call-update) | async-done | bytes 1048592 | tf_op jit(solution)/shard_map/reduce_scatter | solution.py:304
  1031.1 147.7 %reduce-scatter.23.cloned.1.call-done = bf16[2048,256]{1,0:T(8,128)(2,1)} async-done(((bf16[2048,2048]{1,0:T(8,128)(2,1)}), bf16[2048,256]{1,0:T(8,128)(2,1)}) %reduce-scatter.23.cloned.1.call-update) | async-done | bytes 1048592 | tf_op jit(solution)/shard_map/reduce_scatter | solution.py:318
  (219 shorter events, 97.3 us)
Async XLA Ops:
  7.2 6.9 copy-start.3
  7.2 54.8 %all-gather.10.cloned.1.call-start = ((), (), s32[]{:S(2)}) async-start(), calls=%async_computation.9 | async-start | bytes 2359296 | tf_op jit(solution)/shard_map/all_gather | solution.py:217
  7.9 103.8 %all-gather.8.cloned.1.call-start = ((), (), s32[]{:S(2)}) async-start(), calls=%async_computation.8 | async-start | bytes 2359296 | tf_op jit(solution)/shard_map/all_gather | solution.py:216
  8.7 152.9 %all-gather.12.cloned.1.call-start = ((), (), s32[]{:S(2)}) async-start(), calls=%async_computation.10 | async-start | bytes 2359296 | tf_op jit(solution)/shard_map/all_gather | solution.py:218
  9.4 203.0 %all-gather.14.cloned.1.call-start = ((), (), s32[]{:S(2)}) async-start(), calls=%async_computation.11 | async-start | bytes 2359296 | tf_op jit(solution)/shard_map/all_gather | solution.py:222
  10.0 236.4 %all-gather.20.cloned.1.call-start = ((), (), s32[]{:S(2)}) async-start(), calls=%async_computation.15 | async-start | bytes 5242880 | tf_op jit(solution)/shard_map/all_gather | solution.py:256
  10.6 486.0 %all-gather.16.cloned.1.call-start = ((), (), s32[]{:S(2)}) async-start(), calls=%async_computation.12 | async-start | bytes 9437184 | tf_op jit(solution)/shard_map/all_gather | solution.py:219
  11.1 500.0 %all-gather.18.cloned.1.call-start = ((), (), s32[]{:S(2)}) async-start(), calls=%async_computation.13 | async-start | bytes 9437184 | tf_op jit(solution)/shard_map/all_gather | solution.py:223
  14.5 5.6 copy-start.36
  14.5 5.6 copy-start.37
  14.5 6.3 copy-start.38
  17.5 23.5 %collective-permute-start = (bf16[256,2048]{1,0:T(8,128)(2,1)S(1)}, bf16[256,2048]{1,0:T(8,128)(2,1)S(1)}, u32[]{:S(2)}, u32[]{:S(2)}) collective-permute-start(bf16[256,2048]{1,0:T(8,128)(2,1)S(1)} %get-tuple-element.346), channel_id=1, source_target_pairs={{0,1},{1,2},{2,3},{3,0},{4,5},{5,6},{6,7},{7,4},{8,9},{9,10},{10,1... | collective-permute-start | bytes 3145736 | tf_op jit(solution)/shard_map/ppermute | solution.py:206
  18.0 27.0 %collective-permute-start.1 = (bf16[256,2048]{1,0:T(8,128)(2,1)S(1)}, bf16[256,2048]{1,0:T(8,128)(2,1)S(1)}, u32[]{:S(2)}, u32[]{:S(2)}) collective-permute-start(bf16[256,2048]{1,0:T(8,128)(2,1)S(1)} %get-tuple-element.346), channel_id=1, source_target_pairs={{0,3},{1,0},{2,1},{3,2},{4,7},{5,4},{6,5},{7,6},{8,11},{9,8},{10,9... | collective-permute-start | bytes 3145736 | tf_op jit(solution)/shard_map/ppermute | solution.py:211
  20.0 589.5 %reduce-scatter.13.cloned.1.call-start = ((), (), s32[]{:S(2)}) async-start(), calls=%async_computation.17 | async-start | bytes 2359296 | tf_op jit(solution)/shard_map/reduce_scatter | solution.py:286
  41.0 14.2 %collective-permute-start.2 = (bf16[256,2048]{1,0:T(8,128)(2,1)S(1)}, bf16[256,2048]{1,0:T(8,128)(2,1)S(1)}, u32[]{:S(2)}, u32[]{:S(2)}) collective-permute-start(bf16[256,2048]{1,0:T(8,128)(2,1)S(1)} %collective-permute-done), channel_id=1, source_target_pairs={{0,1},{1,2},{2,3},{3,0},{4,5},{5,6},{6,7},{7,4},{8,9},{9,10},{10,1... | collective-permute-start | bytes 3145736 | tf_op jit(solution)/shard_map/ppermute | solution.py:206
  43.9 73.3 %copy-start.18 = (f32[1024,16]{0,1:T(8,128)}, f32[1024,16]{0,1:T(8,128)S(1)}, u32[]{:S(2)}) copy-start(f32[1024,16]{0,1:T(8,128)S(1)} %get-tuple-element.364) | copy-start | bytes 196612
  43.9 73.3 %copy-start.20 = (f32[1024,16]{0,1:T(8,128)}, f32[1024,16]{0,1:T(8,128)S(1)}, u32[]{:S(2)}) copy-start(f32[1024,16]{0,1:T(8,128)S(1)} %get-tuple-element.365) | copy-start | bytes 196612
  111.7 5.5 copy-start.11
  119.5 47.2 %copy-start.12 = (bf16[2,512,8,64]{1,3,2,0:T(8,128)(2,1)S(1)}, bf16[2,512,8,64]{1,3,2,0:T(8,128)(2,1)}, u32[]{:S(2)}) copy-start(bf16[2,512,8,64]{1,3,2,0:T(8,128)(2,1)} %custom-call.3) | copy-start | bytes 3145732
  119.5 47.2 %copy-start.22 = (f32[2,8,512]{2,1,0:T(8,128)S(1)}, f32[2,8,512]{2,1,0:T(8,128)}, u32[]{:S(2)}) copy-start(f32[2,8,512]{2,1,0:T(8,128)} %custom-call.4) | copy-start | bytes 98308
  198.1 48.3 %copy-start.6 = (bf16[2,512,8,64]{1,3,2,0:T(8,128)(2,1)}, bf16[2,512,8,64]{1,3,2,0:T(8,128)(2,1)S(1)}, u32[]{:S(2)}) copy-start(bf16[2,512,8,64]{1,3,2,0:T(8,128)(2,1)S(1)} %get-tuple-element.626) | copy-start | bytes 3145732
  198.1 48.3 %copy-start.13 = (bf16[2,512,8,64]{1,3,2,0:T(8,128)(2,1)}, bf16[2,512,8,64]{1,3,2,0:T(8,128)(2,1)S(1)}, u32[]{:S(2)}) copy-start(bf16[2,512,8,64]{1,3,2,0:T(8,128)(2,1)S(1)} %get-tuple-element.189) | copy-start | bytes 3145732
  320.5 23.6 %copy-start = (f32[1024,8,64]{0,2,1:T(8,128)S(1)}, f32[1024,8,64]{0,2,1:T(8,128)}, u32[]{:S(2)}) copy-start(f32[1024,8,64]{0,2,1:T(8,128)} %get-tuple-element.546) | copy-start | bytes 6291460 | tf_op jit(solution)/shard_map/while/body/eval_jaxpr/while
  417.1 25.1 %copy-start = (f32[1024,8,64]{0,2,1:T(8,128)S(1)}, f32[1024,8,64]{0,2,1:T(8,128)}, u32[]{:S(2)}) copy-start(f32[1024,8,64]{0,2,1:T(8,128)} %get-tuple-element.546) | copy-start | bytes 6291460 | tf_op jit(solution)/shard_map/while/body/eval_jaxpr/while
  451.4 5.1 copy-start.19
  451.4 5.1 copy-start.21
  455.1 5.0 copy-start.8
  459.2 4.9 copy-start.17
  464.0 176.3 %reduce-scatter.15.cloned.1.call-start = ((), (), s32[]{:S(2)}) async-start(), calls=%async_computation.18 | async-start | bytes 2359296 | tf_op jit(solution)/shard_map/reduce_scatter | solution.py:292
  464.0 6.1 copy-start.2
  470.1 241.5 %reduce-scatter.17.cloned.1.call-start = ((), (), s32[]{:S(2)}) async-start(), calls=%async_computation.19 | async-start | bytes 2359296 | tf_op jit(solution)/shard_map/reduce_scatter | solution.py:298
  471.0 6.1 copy-start.33
  471.0 6.1 copy-start.14
  477.0 306.1 %reduce-scatter.19.cloned.1.call-start = ((), (), s32[]{:S(2)}) async-start(), calls=%async_computation.20 | async-start | bytes 2359296 | tf_op jit(solution)/shard_map/reduce_scatter | solution.py:312
  483.0 346.1 %reduce-scatter.11.cloned.1.call-start = ((), (), s32[]{:S(2)}) async-start(), calls=%async_computation.16 | async-start | bytes 5242880 | tf_op jit(solution)/shard_map/reduce_scatter | solution.py:282
  483.3 7.7 copy-start.16
  483.3 7.7 copy-start.41
  531.8 14.0 %copy-start.5 = (f32[1024,2048]{1,0:T(8,128)S(1)}, f32[1024,2048]{1,0:T(8,128)}, u32[]{:S(2)}) copy-start(f32[1024,2048]{1,0:T(8,128)} %fusion.95) | copy-start | bytes 25165828
  557.3 319.0 %reduce-scatter.9.cloned.1.call-start = ((), (), s32[]{:S(2)}) async-start(), calls=%async_computation.14 | async-start | bytes 5242880 | tf_op jit(solution)/shard_map/reduce_scatter | solution.py:251
  557.3 16.1 %copy-start.40 = (bf16[512,2048]{1,0:T(8,128)(2,1)S(1)}, bf16[512,2048]{1,0:T(8,128)(2,1)}, u32[]{:S(2)}) copy-start(bf16[512,2048]{1,0:T(8,128)(2,1)} %all-gather.14.cloned.1.call-done) | copy-start | bytes 6291460
  577.8 450.4 %reduce-scatter.21.cloned.1.call-start = ((), (), s32[]{:S(2)}) async-start(), calls=%async_computation.21 | async-start | bytes 9437184 | tf_op jit(solution)/shard_map/reduce_scatter | solution.py:304
  592.2 586.6 %reduce-scatter.23.cloned.1.call-start = ((), (), s32[]{:S(2)}) async-start(), calls=%async_computation.22 | async-start | bytes 9437184 | tf_op jit(solution)/shard_map/reduce_scatter | solution.py:318
  608.5 220.6 %copy-start.4 = (bf16[256,2048]{1,0:T(8,128)(2,1)S(1)}, bf16[256,2048]{1,0:T(8,128)(2,1)}, u32[]{:S(2)}) copy-start(bf16[256,2048]{1,0:T(8,128)(2,1)} %param.21) | copy-start | bytes 3145732
  608.5 220.6 %copy-start.24 = (f32[2048]{0:T(1024)S(1)}, f32[2048]{0:T(1024)}, u32[]{:S(2)}) copy-start(f32[2048]{0:T(1024)} %copy-done.23) | copy-start | bytes 24580
  608.5 220.6 %copy-start.26 = (f32[256]{0:T(256)S(1)}, f32[256]{0:T(256)}, u32[]{:S(2)}) copy-start(f32[256]{0:T(256)} %copy-done.25) | copy-start | bytes 3076
  608.5 220.6 %copy-start.31 = (f32[256]{0:T(256)S(1)}, f32[256]{0:T(256)}, u32[]{:S(2)}) copy-start(f32[256]{0:T(256)} %copy-done.30) | copy-start | bytes 3076
  609.2 267.1 %copy-start.9 = (bf16[256,2048]{1,0:T(8,128)(2,1)S(1)}, bf16[256,2048]{1,0:T(8,128)(2,1)}, u32[]{:S(2)}) copy-start(bf16[256,2048]{1,0:T(8,128)(2,1)} %param.37) | copy-start | bytes 3145732
  923.8 258.3 %copy-start.32 = (f32[2048]{0:T(1024)}, f32[2048]{0:T(1024)S(1)}, u32[]{:S(2)}) copy-start(f32[2048]{0:T(1024)S(1)} %get-tuple-element.603) | copy-start | bytes 24580
  (15 other events, 23.1 us)
Sparse Core Ops, SparseCore 0:
  10.1 51.7 all-gather.9
  64.1 47.6 all-gather.7
  113.9 47.6 all-gather.11
  163.4 48.9 all-gather.13
  213.8 32.5 all-gather.19
  248.4 124.4 all-gather.15
  374.9 123.1 all-gather.17
  502.2 66.5 reduce-scatter.12
  572.9 67.3 reduce-scatter.14
  644.2 67.3 reduce-scatter.16
  715.1 67.9 reduce-scatter.18
  785.5 43.5 reduce-scatter.10
  831.6 44.5 reduce-scatter.8
  879.7 148.5 reduce-scatter.20
  1031.8 146.9 reduce-scatter.22
